TPU v7x, 32 devices: a whole 2x2x4 slice. The times are simulated.
32 devices in a mesh: blk: 4 (over y, x), grp: 8 (over z, core).
Axes of the slice: x: 2, y: 2, z: 4, core: 2. Of those that a mesh axis runs over, the one named last changes fastest.
Arguments:
- points: float32 [3, 4096], P(None, ('blk', 'grp')), may hold values from 0 to 1
- labels: int32 [4096], P(('blk', 'grp')), may hold values 0 or 1
- shape_scale: float32 [4096], P(('blk', 'grp')), may hold values from 0.1 to 0.4
- krylov_basis: float32 [8, 32, 4096], P(None, None, ('blk', 'grp')), may hold values from -6 to 6
- sketch: float32 [1024, 4096], P(None, ('blk', 'grp')), may hold values from -0.09375 to 0.09375
- sketched_basis: float32 [8, 32, 1024], replicated, may hold values from -0.1875 to 0.1875
Outputs:
- next_vector: float32 [32, 4096], P(None, ('blk', 'grp'))
- coefficients: float32 [8, 32], replicated
- sketch_next: float32 [32, 1024], replicated
- norms: float32 [32], replicated
All inputs are finite; a program needn't handle non-finite values. No bound on the sum of `labels` on one device may be relied on, other than what follows from the above.
Results may differ from a plain program's by a relative error of at most 0.0003.
Values sent between devices are 32-bit elements; how exact they have to be, the bound alone decides.
A program may use at most 64 MiB of HBM per device.

v0:
```python
import math

import jax
import jax.numpy as jnp
from jax import lax
from jax.sharding import PartitionSpec as P

SYSTEMS = 32
KRYLOV = 8


def kernel_terms(target_points, target_labels, source_block):
    source_points = source_block[0:3]
    scales = source_block[3]
    weights_block = source_block[4:]
    delta_x = source_points[0][:, None] - target_points[0][None, :]
    delta_y = source_points[1][:, None] - target_points[1][None, :]
    delta_z = source_points[2][:, None] - target_points[2][None, :]
    radius_sq = delta_x * delta_x + delta_y * delta_y + delta_z * delta_z
    squared_scale = (scales * scales)[:, None]
    shifted = radius_sq + squared_scale
    inverse = lax.rsqrt(shifted)
    boundary = shifted * inverse
    interior = (3.0 * squared_scale + 2.0 * radius_sq) * inverse * inverse * inverse
    kernel = jnp.where(target_labels[None, :] == 1, interior, boundary)
    return jnp.dot(
        weights_block, kernel, precision=lax.Precision.HIGHEST, preferred_element_type=jnp.float32
    )


def block_size(length, wanted):
    return wanted if length % wanted == 0 else length


def accumulate(running, target_points, target_labels, source_block):
    target_count = target_points.shape[1]
    source_count = source_block.shape[1]
    tblock = block_size(target_count, 2048)
    sblock = block_size(source_count, 2048)
    system_rows = running.shape[0]

    def over_targets(target_index, current):

        def over_sources(source_index, partial_value):
            portion = lax.dynamic_slice_in_dim(source_block, source_index * sblock, sblock, 1)
            return partial_value + kernel_terms(target_points, target_labels, portion)

        partial_value = lax.fori_loop(
            0, source_count // sblock, over_sources, jnp.zeros((system_rows, tblock), jnp.float32)
        )
        return current + partial_value

    return lax.fori_loop(0, target_count // tblock, over_targets, running)


def shards(points, labels, shape_scale, krylov_basis, sketch, sketched_basis):
    own_count = points.shape[1]
    everything = lax.axis_size("blk") * lax.axis_size("grp") * own_count
    sources = jnp.concatenate([points, shape_scale[None, :], krylov_basis[KRYLOV - 1]], axis=0)
    empty = jnp.zeros((SYSTEMS, own_count), jnp.float32)
    summed = accumulate(
        empty, points, labels, lax.all_gather(sources, ("blk", "grp"), axis=1, tiled=True)
    )
    image = summed / math.sqrt(everything)
    local_sketch = lax.dot_general(
        image,
        sketch,
        (((1,), (1,)), ((), ())),
        precision=lax.Precision.HIGHEST,
        preferred_element_type=jnp.float32,
    )
    sketched = lax.psum(local_sketch, ("blk", "grp"))
    coefficients = jnp.einsum(
        "jrk,rk->jr", sketched_basis, sketched, precision=lax.Precision.HIGHEST
    )
    remainder = sketched - jnp.einsum(
        "jr,jrk->rk", coefficients, sketched_basis, precision=lax.Precision.HIGHEST
    )
    norms = jnp.sqrt(jnp.mean(remainder * remainder, axis=1) + 1e-06)
    sketch_next = remainder / norms[:, None]
    reduced = image - jnp.einsum(
        "jr,jrn->rn", coefficients, krylov_basis, precision=lax.Precision.HIGHEST
    )
    next_vector = reduced / norms[:, None]
    return (next_vector, coefficients, sketch_next, norms)


def solution(mesh):
    placed = (
        P(None, ("blk", "grp")),
        P(("blk", "grp")),
        P(("blk", "grp")),
        P(None, None, ("blk", "grp")),
        P(None, ("blk", "grp")),
        P(),
    )
    return jax.shard_map(
        shards,
        mesh=mesh,
        in_specs=placed,
        out_specs=(P(None, ("blk", "grp")), P(), P(), P()),
        check_vma=False,
    )
```

profile of v0, /device:TPU:0, one launch (start us, length us, event | category | flops | bytes accessed | tf_op | source)
XLA Modules:
  0.0 195.9 jit_solution(17373773227067051160)
XLA Ops:
  7.2 0.0 copy-start
  7.2 0.0 all-reduce.2.cloned.1.call-start
  7.2 0.0 copy-start.4
  7.2 0.8 slice_bitcast_fusion.3
  8.0 0.0 copy-start.7
  8.1 0.0 copy-done.4
  8.1 0.7 copy-done.7
  8.7 45.9 %all_gather.3 = f32[36,4096]{1,0:T(8,128)S(1)} all-gather(f32[36,128]{1,0:T(8,128)S(1)} %pad_maximum_fusion), channel_id=1, replica_groups=mesh['blk'=4,'grp'=8] {'blk','grp'}, dimensions={1}, use_global_device_ids=true | all-gather | bytes 608256 | tf_op jit(solution)/shard_map/all_gather | solution.py:62
  54.7 0.0 copy-done.8
  54.7 4.4 %while.21 = (s32[]{:T(128)}, f32[32,128]{1,0:T(8,128)S(1)}, f32[36,4096]{1,0:T(8,128)S(1)}, s32[128]{0:T(128)S(1)}, f32[3,128]{1,0:T(4,128)S(1)}, /*index=5*/s32...) while((s32[]{:T(128)}, f32[32,128]{1,0:T(8,128)S(1)}, ...), condition=%wide.region_1.0_spmd.clone, body=%wide.region_0.1_spmd.clone.sunk | while | flops 104870024 | bytes 423813 | solution.py:48
  54.7 0.1 constant_dynamic-slice_fusion.2
  54.8 2.0 %convolution_add_fusion.2 = f32[32,128]{1,0:T(8,128)S(1)} fusion(f32[2048]{0:T(1024)S(1)} %bitcast.42, f32[128]{0:T(128)S(1)} %get-tuple-element.195, f32[2048]{0:T(1024)S(1)} %bitcast.45, f32[128]{0:T(128)S(1)} %get-tuple-element.197, f32[2048]{0:T(1024)S(1)} %bitcast.44, f32[128]{0:T(128)S(1)} %get-tuple-element.199, f32[2048]{0:T(1024)S(1)} %bitcast.43, ...), kind=kOutput, calls=%fused_computation.2.clone.1 | convolution fusion | flops 104865792 | bytes 337929 | tf_op jit(solution)/shard_map/while/body/eval_jaxpr/while/body/eval_jaxpr/dot_general | solution.py:26
  56.9 0.1 constant_dynamic-slice_fusion.2
  57.0 2.0 %convolution_add_fusion.2 = f32[32,128]{1,0:T(8,128)S(1)} fusion(f32[2048]{0:T(1024)S(1)} %bitcast.42, f32[128]{0:T(128)S(1)} %get-tuple-element.195, f32[2048]{0:T(1024)S(1)} %bitcast.45, f32[128]{0:T(128)S(1)} %get-tuple-element.197, f32[2048]{0:T(1024)S(1)} %bitcast.44, f32[128]{0:T(128)S(1)} %get-tuple-element.199, f32[2048]{0:T(1024)S(1)} %bitcast.43, ...), kind=kOutput, calls=%fused_computation.2.clone.1 | convolution fusion | flops 104865792 | bytes 337929 | tf_op jit(solution)/shard_map/while/body/eval_jaxpr/while/body/eval_jaxpr/dot_general | solution.py:26
  59.1 0.0 copy-done.2
  59.1 1.3 fusion.32
  60.3 0.0 all-reduce.2.cloned.1.call-update
  60.4 120.9 %all-reduce.2.cloned.1.call-done = f32[32,1024]{1,0:T(8,128)} async-done(((f32[32,1024]{1,0:T(8,128)}), f32[32,1024]{1,0:T(8,128)}) %all-reduce.2.cloned.1.call-update) | async-done | bytes 131088 | tf_op jit(solution)/shard_map/psum | solution.py:72
  181.2 0.0 copy-done
  181.3 3.6 %fusion.27 = f32[32,1,8]{2,1,0:T(1,128)S(1)} fusion(f32[8,32,1024]{2,1,0:T(8,128)S(1)} %copy-done, f32[32,1024,1]{1,0,2:T(8,128)} %bitcast.40), kind=kOutput, calls=%fused_computation.36 | convolution fusion | flops 3145728 | bytes 1180672 | tf_op jit(solution)/shard_map/jrk,rk->jr/dot_general | solution.py:73
  184.8 0.1 copy.12
  184.9 0.1 copy.13
  185.0 0.5 copy-done.5
  185.5 0.0 copy-done.3
  185.5 0.4 fusion.29
  185.9 0.0 copy-start.1
  185.9 1.5 fusion.25
  187.4 0.0 copy-done.1
  187.4 0.1 multiply_reduce_fusion
  187.6 0.7 subtract_divide_fusion
  188.3 0.0 copy-done.6
  188.3 0.7 broadcast_divide_fusion
  (14 shorter events, 0.1 us)
Async XLA Ops:
  7.2 174.1 %copy-start = (f32[8,32,1024]{2,1,0:T(8,128)S(1)}, f32[8,32,1024]{2,1,0:T(8,128)}, u32[]{:S(2)}) copy-start(f32[8,32,1024]{2,1,0:T(8,128)} %param.13) | copy-start | bytes 3145732
  7.2 174.1 %all-reduce.2.cloned.1.call-start = ((), (), s32[]{:S(2)}) async-start(), calls=%async_computation | async-start | bytes 262144 | tf_op jit(solution)/shard_map/psum | solution.py:72
  7.2 0.8 copy-start.4
  8.0 0.7 copy-start.7
  8.7 46.0 %copy-start.8 = (s32[128]{0:T(128)S(1)}, s32[128]{0:T(128)}, u32[]{:S(2)}) copy-start(s32[128]{0:T(128)} %param.9) | copy-start | bytes 1540
  54.7 4.4 %copy-start.2 = (f32[1024,128]{1,0:T(8,128)S(1)}, f32[1024,128]{1,0:T(8,128)}, u32[]{:S(2)}) copy-start(f32[1024,128]{1,0:T(8,128)} %param.12) | copy-start | bytes 1572868
  181.2 4.3 %copy-start.3 = (f32[8,32,128]{2,1,0:T(8,128)S(1)}, f32[8,32,128]{2,1,0:T(8,128)}, u32[]{:S(2)}) copy-start(f32[8,32,128]{2,1,0:T(8,128)} %param.11) | copy-start | bytes 393220
  184.9 0.6 copy-start.5
  185.9 1.5 copy-start.1
  187.6 0.7 copy-start.6
Sparse Core Ops, SparseCore 0:
  60.5 120.7 all-reduce.1
where the time goes:
time: 196 us
  waiting for transfers between devices  121 us (62%)
  blocking collectives  45.9 us (23%)
  between operations  14.1 us (7%)
  matrix products  10.7 us (5%)
  local copies, waits for them, and re-layouts  2.17 us (1%)
    psum x1, waiting for transfers between devices, shards(): sketched = lax.psum(local_sketch, ('blk', 'grp'))  121 us
    all_gather x1, blocking collectives, shards(): lax.all_gather(sources, ('blk', 'grp'), axis=1, tiled=True)  45.9 us
    dot_general x2, matrix products, kernel_terms(): jnp.dot(weights_block, kernel, precision=lax.Precision.HIGHEST, preferred...  4 us
  transfers between devices with their start and end apart: 1, of which 1 were waited for; matrix products, arithmetic and copies ran while one was open for 0% of the time, Pallas kernels for 0%

commit v1 on v0

v1 whole, which is shorter than its diff:
```python
import functools
import math

import jax
import jax.numpy as jnp
from jax import lax
from jax.experimental import pallas as pl
from jax.experimental.pallas import tpu as pltpu
from jax.sharding import PartitionSpec as P

MESH = pl.DeviceIdType.MESH
F32 = jnp.float32
BF16 = jnp.bfloat16
NT = (((1,), (1,)), ((), ()))


def split(value):
    high = value.astype(BF16)
    low = (value - high.astype(F32)).astype(BF16)
    return high, low


def nt_dot(left, right):
    return lax.dot_general(left, right, NT, preferred_element_type=F32)


def step_kernel(
    nb, ng,
    points_hbm, labels_hbm, scale_hbm, krylov_hbm, sketch_hbm, basis_hbm,
    next_ref, coef_ref, sketch_next_ref, norms_ref,
    pts, lab, scl, krylov, sketch, basis,
    geo, src_geo, tgt_geo, weights,
    tgx, tgy, tgz, tgl, k_high, k_low, w_cat, acc,
    part, part_in, image_ref, sk_high, sk_low,
    sk_part, sk_in, sk_full, cmat,
    local_sem, geo_send, geo_recv, w_send, w_recv, tgt_send, tgt_recv,
    img_send, img_recv, rs_send, rs_recv, ag_send, ag_recv,
):
    b = lax.axis_index("blk")
    g = lax.axis_index("grp")
    ndev = nb * ng
    me = b * ng + g
    own = pts.shape[1]
    vectors, systems, _ = krylov.shape
    tiles = sk_part.shape[0]
    row_groups = systems // 8
    col_blocks = tiles // row_groups

    def at(d):
        return (d // ng, lax.rem(d, ng))

    def remote(src, dst, send, recv, where):
        return pltpu.make_async_remote_copy(
            src_ref=src, dst_ref=dst, send_sem=send, recv_sem=recv,
            device_id=where, device_id_type=MESH,
        )

    copies = [
        pltpu.make_async_copy(points_hbm, pts, local_sem.at[0]),
        pltpu.make_async_copy(labels_hbm, lab, local_sem.at[1]),
        pltpu.make_async_copy(scale_hbm, scl, local_sem.at[2]),
        pltpu.make_async_copy(krylov_hbm.at[vectors - 1], weights.at[g], local_sem.at[3]),
        pltpu.make_async_copy(sketch_hbm, sketch, local_sem.at[4]),
        pltpu.make_async_copy(krylov_hbm, krylov, local_sem.at[5]),
        pltpu.make_async_copy(basis_hbm, basis, local_sem.at[6]),
    ]
    for copy in copies:
        copy.start()

    barrier = pltpu.get_barrier_semaphore()

    def greet(i, carry):
        pl.semaphore_signal(
            barrier, inc=1, device_id=at(lax.rem(me + i, ndev)), device_id_type=MESH
        )
        return carry

    lax.fori_loop(1, ndev, greet, 0)

    for copy in copies[:3]:
        copy.wait()
    scale = scl[...]
    mine = jnp.concatenate(
        [pts[...], scale * scale, lab[...].astype(F32), jnp.zeros((3, own), F32)], axis=0
    )
    geo[...] = mine
    src_geo[g] = mine
    tgt_geo[b] = mine
    copies[3].wait()
    pl.semaphore_wait(barrier, ndev - 1)

    def geo_copy(peer, slot):
        return remote(geo, src_geo.at[slot], geo_send.at[peer], geo_recv.at[slot], (b, peer))

    def tgt_copy(peer, slot):
        return remote(geo, tgt_geo.at[slot], tgt_send.at[peer], tgt_recv.at[slot], (peer, g))

    def w_copy(peer, slot):
        return remote(
            weights.at[g], weights.at[slot], w_send.at[peer], w_recv.at[slot], (b, peer)
        )

    def over(count, first, self_index, action):
        def step(i, carry):
            action(lax.rem(self_index + i, count))
            return carry

        lax.fori_loop(first, count, step, 0)

    over(nb, 1, b, lambda p: tgt_copy(p, b).start())
    over(ng, 1, g, lambda p: geo_copy(p, g).start())
    over(ng, 1, g, lambda p: w_copy(p, g).start())

    copies[4].wait()
    high, low = split(sketch[...])
    sk_high[...] = high
    sk_low[...] = low

    over(nb, 1, b, lambda p: tgt_copy(p, p).wait_recv())
    for k in range(nb):
        turned = jnp.transpose(tgt_geo[k])
        rows = pl.ds(k * own, own)
        tgx[rows, :] = jnp.broadcast_to(turned[:, 0:1], (own, own))
        tgy[rows, :] = jnp.broadcast_to(turned[:, 1:2], (own, own))
        tgz[rows, :] = jnp.broadcast_to(turned[:, 2:3], (own, own))
        tgl[rows, :] = jnp.broadcast_to(turned[:, 4:5], (own, own))

    def columns(p):
        return pl.ds(pl.multiple_of(p * own, own), own)

    def kernel_block(i, carry):
        p = lax.rem(g + i, ng)

        @pl.when(i > 0)
        def _():
            geo_copy(p, p).wait_recv()

        block = src_geo[p]
        sx, sy, sz, ss = block[0:1], block[1:2], block[2:3], block[3:4]
        for first in range(0, nb * own, 32):
            rows = pl.ds(first, 32)
            dx = sx - tgx[rows, :]
            dy = sy - tgy[rows, :]
            dz = sz - tgz[rows, :]
            q = dx * dx + dy * dy + dz * dz + ss
            inverse = lax.rsqrt(q)
            interior = (q + q + ss) * (inverse * inverse)
            value = jnp.where(tgl[rows, :] > 0.5, interior, q) * inverse
            value_high, value_low = split(value)
            k_high[rows, columns(p)] = value_high
            k_low[rows, columns(p)] = value_low
        return carry

    lax.fori_loop(0, ng, kernel_block, 0)

    def weight_block(i, carry):
        p = lax.rem(g + i, ng)

        @pl.when(i > 0)
        def _():
            w_copy(p, p).wait_recv()

        w_high, w_low = split(weights[p])
        w_cat[0:systems, columns(p)] = w_high
        w_cat[systems : 2 * systems, columns(p)] = w_low
        return carry

    lax.fori_loop(0, ng, weight_block, 0)

    width = min(ng, 8) * own
    chunks = (ng * own) // width

    def product(c):
        cols = pl.ds(pl.multiple_of(c * width, width), width)
        both = nt_dot(w_cat[:, cols], k_high[:, cols])
        rest = nt_dot(w_cat[0:systems, cols], k_low[:, cols])
        return both[0:systems] + both[systems:] + rest

    if chunks == 1:
        total = product(0)
    else:
        acc[...] = jnp.zeros_like(acc)

        def add_chunk(c, carry):
            acc[...] += product(c)
            return carry

        lax.fori_loop(0, chunks, add_chunk, 0)
        total = acc[...]
    for k in range(nb):
        part[k] = total[:, k * own : (k + 1) * own]

    def img_copy(peer, slot):
        return remote(
            part.at[peer], part_in.at[slot], img_send.at[peer], img_recv.at[slot], (peer, g)
        )

    over(nb, 1, b, lambda p: img_copy(p, b).start())
    part_in[b] = part[b]
    over(nb, 1, b, lambda p: img_copy(p, p).wait_recv())
    image = part_in[0]
    for k in range(1, nb):
        image = image + part_in[k]
    image = image * (1.0 / math.sqrt(ndev * own))
    image_ref[...] = image

    image_high, image_low = split(image)
    image_cat = jnp.concatenate([image_high, image_low], axis=0)
    both = nt_dot(image_cat, sk_high[...])
    rest = nt_dot(image_high, sk_low[...])
    local = both[0:systems] + both[systems:] + rest
    for r in range(row_groups):
        for c in range(col_blocks):
            sk_part[r * col_blocks + c] = local[r * 8 : r * 8 + 8, c * 128 : c * 128 + 128]

    tile = lax.rem(me, tiles)
    base = me - tile

    def rs_copy(peer, slot):
        return remote(
            sk_part.at[lax.rem(peer, tiles)], sk_in.at[slot],
            rs_send.at[peer], rs_recv.at[slot], at(peer),
        )

    def ag_copy(peer, slot):
        return remote(
            sk_full.at[tile], sk_full.at[slot], ag_send.at[peer], ag_recv.at[slot], at(base + peer)
        )

    over(ndev, 1, me, lambda p: rs_copy(p, me).start())
    sk_in[me] = sk_part[tile]
    copies[5].wait()
    copies[6].wait()
    over(ndev, 1, me, lambda p: rs_copy(p, p).wait_recv())

    reach = min(ndev, 32)

    def add_tiles(i, value):
        for k in range(reach):
            value = value + sk_in[i * reach + k]
        return value

    if ndev == reach:
        summed = add_tiles(0, jnp.zeros((8, 128), F32))
    else:
        summed = lax.fori_loop(0, ndev // reach, add_tiles, jnp.zeros((8, 128), F32))
    sk_full[tile] = summed
    over(tiles, 1, tile, lambda p: ag_copy(p, tile).start())
    over(tiles, 1, tile, lambda p: ag_copy(p, p).wait_recv())

    lanes = lax.broadcasted_iota(jnp.int32, (8, 128), 1)
    for r in range(row_groups):
        rows = pl.ds(r * 8, 8)
        rest = [sk_full[r * col_blocks + c] for c in range(col_blocks)]
        coefs = []
        table = jnp.zeros((8, 128), F32)
        for j in range(vectors):
            run = rest[0] * basis[j, rows, 0:128]
            for c in range(1, col_blocks):
                run = run + rest[c] * basis[j, rows, c * 128 : c * 128 + 128]
            value = jnp.sum(run, axis=1, keepdims=True)
            coefs.append(value)
            table = jnp.where(lanes == j, value, table)
        squares = jnp.zeros((8, 128), F32)
        left = []
        for c in range(col_blocks):
            value = rest[c]
            for j in range(vectors):
                value = value - coefs[j] * basis[j, rows, c * 128 : c * 128 + 128]
            squares = squares + value * value
            left.append(value)
        mean = jnp.sum(squares, axis=1, keepdims=True) * (1.0 / (col_blocks * 128))
        norm = jnp.sqrt(mean + 1e-06)
        inverse = 1.0 / norm
        for c in range(col_blocks):
            sketch_next_ref[rows, c * 128 : c * 128 + 128] = left[c] * inverse
        vector = image_ref[rows, :]
        for j in range(vectors):
            vector = vector - coefs[j] * krylov[j, rows, :]
        next_ref[rows, :] = vector * inverse
        cmat[rows, :] = jnp.where(lanes == vectors, norm, table)
    turned = jnp.transpose(cmat[...])
    coef_ref[...] = turned[0:vectors, :]
    norms_ref[...] = turned[vectors : vectors + 1, :]

    over(nb, 1, b, lambda p: tgt_copy(p, b).wait_send())
    over(ng, 1, g, lambda p: geo_copy(p, g).wait_send())
    over(ng, 1, g, lambda p: w_copy(p, g).wait_send())
    over(nb, 1, b, lambda p: img_copy(p, b).wait_send())
    over(ndev, 1, me, lambda p: rs_copy(p, me).wait_send())
    over(tiles, 1, tile, lambda p: ag_copy(p, tile).wait_send())


def shards(nb, ng, points, labels, shape_scale, krylov_basis, sketch, sketched_basis):
    own = points.shape[1]
    vectors, systems, _ = krylov_basis.shape
    sketch_rows = sketch.shape[0]
    ndev = nb * ng
    tiles = (systems // 8) * (sketch_rows // 128)
    assert ndev % tiles == 0
    vmem = pltpu.VMEM
    dma = pltpu.SemaphoreType.DMA
    hbm = pl.BlockSpec(memory_space=pl.ANY)
    out = pl.BlockSpec(memory_space=pltpu.VMEM)
    next_vector, coefficients, sketch_next, norms = pl.pallas_call(
        functools.partial(step_kernel, nb, ng),
        out_shape=(
            jax.ShapeDtypeStruct((systems, own), F32),
            jax.ShapeDtypeStruct((vectors, systems), F32),
            jax.ShapeDtypeStruct((systems, sketch_rows), F32),
            jax.ShapeDtypeStruct((1, systems), F32),
        ),
        in_specs=[hbm] * 6,
        out_specs=(out,) * 4,
        scratch_shapes=[
            vmem((3, own), F32), vmem((1, own), jnp.int32), vmem((1, own), F32),
            vmem(krylov_basis.shape, F32), vmem(sketch.shape, F32), vmem(sketched_basis.shape, F32),
            vmem((8, own), F32), vmem((ng, 8, own), F32), vmem((nb, 8, own), F32),
            vmem((ng, systems, own), F32),
            vmem((nb * own, own), F32), vmem((nb * own, own), F32),
            vmem((nb * own, own), F32), vmem((nb * own, own), F32),
            vmem((nb * own, ng * own), BF16), vmem((nb * own, ng * own), BF16),
            vmem((2 * systems, ng * own), BF16), vmem((systems, nb * own), F32),
            vmem((nb, systems, own), F32), vmem((nb, systems, own), F32), vmem((systems, own), F32),
            vmem(sketch.shape, BF16), vmem(sketch.shape, BF16),
            vmem((tiles, 8, 128), F32), vmem((ndev, 8, 128), F32), vmem((tiles, 8, 128), F32),
            vmem((systems, 128), F32),
            dma((7,)), dma((ng,)), dma((ng,)), dma((ng,)), dma((ng,)), dma((nb,)), dma((nb,)),
            dma((nb,)), dma((nb,)), dma((ndev,)), dma((ndev,)), dma((tiles,)), dma((tiles,)),
        ],
        compiler_params=pltpu.CompilerParams(
            collective_id=0, has_side_effects=True, vmem_limit_bytes=48 * 1024 * 1024
        ),
    )(
        points, labels.reshape(1, own), shape_scale.reshape(1, own),
        krylov_basis, sketch, sketched_basis,
    )
    return (next_vector, coefficients, sketch_next, norms.reshape(systems))


def solution(mesh):
    placed = (
        P(None, ("blk", "grp")),
        P(("blk", "grp")),
        P(("blk", "grp")),
        P(None, None, ("blk", "grp")),
        P(None, ("blk", "grp")),
        P(),
    )
    return jax.shard_map(
        functools.partial(shards, mesh.shape["blk"], mesh.shape["grp"]),
        mesh=mesh,
        in_specs=placed,
        out_specs=(P(None, ("blk", "grp")), P(), P(), P()),
        check_vma=False,
    )
```

time: 196 us -> 37.1 us (0.19)
  waiting for transfers between devices: 121 us -> 0 us
  blocking collectives: 45.9 us -> 0 us
  Pallas kernels: 0 us -> 30 us
  between operations: 14.1 us -> 0.67 us
  matrix products: 10.7 us -> 0 us
  local copies, waits for them, and re-layouts: 2.17 us -> 6.2 us
    psum x1 -> x0, waiting for transfers between devices: 121 us -> none  [shards(): sketched = lax.psum(local_sketch, ('blk', 'grp'))]
    all_gather x1 -> x0, blocking collectives: 45.9 us -> none  [shards(): lax.all_gather(sources, ('blk', 'grp'), axis=1, tiled=True)]
    pallas_call x0 -> x1, Pallas kernels: none -> 30 us  [shards(): pl.pallas_call(functools.partial(step_kernel, nb, ng), out_shape=(jax.Sha...]
    dot_general x6 -> x0, matrix products: 10.7 us -> none  [the longest x2 4 us: kernel_terms(): jnp.dot(weights_block, kernel, precision=lax.Precision.HIGHEST, preferred...]
    unnamed x18 -> x16, local copies, waits for them, and re-layouts: 1.22 us -> 6.2 us
  transfers between devices with their start and end apart: 1 -> 0, of which waited for: 1 -> 0; matrix products, arithmetic and copies ran while one was open for 0% -> 0% of each run, Pallas kernels for 0% -> 0%
where the time goes in v1:
time: 37.1 us; the launch traced here: 36.8 us
  Pallas kernels  30 us (81%)
  local copies, waits for them, and re-layouts  6.2 us (17%)
  between operations  0.67 us (2%)
    pallas_call x1, Pallas kernels, shards(): pl.pallas_call(functools.partial(step_kernel, nb, ng), out_shape=(jax.Sha...  30 us
    unnamed x16, local copies, waits for them, and re-layouts  6.2 us

profile of v1, /device:TPU:0, one launch (start us, length us, event | category | flops | bytes accessed | tf_op | source)
XLA Modules:
  0.0 36.8 jit_solution(46153325649874452)
XLA Ops:
  0.6 0.0 copy-start.3
  0.6 0.0 copy-start.4
  0.7 0.0 copy-start.5
  0.7 0.7 %copy-done.3 = f32[3,128]{1,0:T(4,128)S(1)} copy-done((f32[3,128]{1,0:T(4,128)S(1)}, f32[3,128]{1,0:T(4,128)}, u32[]{:S(2)}) %copy-start.3) | copy-done | bytes 1560
  1.3 0.0 copy-done.4
  1.3 0.0 copy-done.5
  1.3 0.0 copy-start
  1.3 1.2 %copy-done = f32[8,32,1024]{2,1,0:T(8,128)S(1)} copy-done((f32[8,32,1024]{2,1,0:T(8,128)S(1)}, f32[8,32,1024]{2,1,0:T(8,128)}, u32[]{:S(2)}) %copy-start) | copy-done | bytes 1048600
  2.5 0.0 copy-start.1
  2.5 1.0 %copy-done.1 = f32[1024,128]{1,0:T(8,128)S(1)} copy-done((f32[1024,128]{1,0:T(8,128)S(1)}, f32[1024,128]{1,0:T(8,128)}, u32[]{:S(2)}) %copy-start.1) | copy-done | bytes 524312
  3.6 0.0 copy-start.2
  3.6 0.9 %copy-done.2 = f32[8,32,128]{2,1,0:T(8,128)S(1)} copy-done((f32[8,32,128]{2,1,0:T(8,128)S(1)}, f32[8,32,128]{2,1,0:T(8,128)}, u32[]{:S(2)}) %copy-start.2) | copy-done | bytes 131096
  4.5 30.0 %shard_map.93 = (f32[32,128]{1,0:T(8,128)S(1)}, f32[8,32]{1,0:T(8,128)S(1)}, f32[32,1024]{1,0:T(8,128)S(1)}, f32[1,32]{1,0:T(1,128)S(1)}) custom-call(f32[3,128]{1,0:T(4,128)S(1)} %copy-done.3, s32[1,128]{1,0:T(1,128)S(1)} %bitcast.3, f32[1,128]{1,0:T(1,128)S(1)} %bitcast.4, f32[8,32,128]{2,1,0:T(8,128)S(1)} %copy-done.2, f32[1024,128]{1,0:T(8,128)S(1)} %copy-done.1, ...), custom_call_target="tpu_custom_call" | custom-call | tf_op jit(solution)/shard_map/pallas_call | solution.py:305
  34.5 0.6 %copy.14 = f32[32,128]{1,0:T(8,128)} copy(f32[32,128]{1,0:T(8,128)S(1)} %get-tuple-element.16) | data formatting | bytes 32768
  35.1 0.6 %copy.15 = f32[8,32]{1,0:T(8,128)} copy(f32[8,32]{1,0:T(8,128)S(1)} %get-tuple-element.17) | data formatting | bytes 2048
  35.7 0.7 %copy.16 = f32[32,1024]{1,0:T(8,128)} copy(f32[32,1024]{1,0:T(8,128)S(1)} %get-tuple-element.18) | data formatting | bytes 262144
  36.3 0.5 %copy.17 = f32[32]{0:T(128)} copy(f32[32]{0:T(128)S(1)} %bitcast.5) | data formatting | bytes 256
Async XLA Ops:
  0.6 0.7 %copy-start.3 = (f32[3,128]{1,0:T(4,128)S(1)}, f32[3,128]{1,0:T(4,128)}, u32[]{:S(2)}) copy-start(f32[3,128]{1,0:T(4,128)} %points_hbm.1) | copy-start | bytes 4612
  0.6 0.7 %copy-start.4 = (s32[128]{0:T(128)S(1)}, s32[128]{0:T(128)}, u32[]{:S(2)}) copy-start(s32[128]{0:T(128)} %param.7) | copy-start | bytes 1540
  0.7 0.7 %copy-start.5 = (f32[128]{0:T(128)S(1)}, f32[128]{0:T(128)}, u32[]{:S(2)}) copy-start(f32[128]{0:T(128)} %param.8) | copy-start | bytes 1540
  1.3 1.2 %copy-start = (f32[8,32,1024]{2,1,0:T(8,128)S(1)}, f32[8,32,1024]{2,1,0:T(8,128)}, u32[]{:S(2)}) copy-start(f32[8,32,1024]{2,1,0:T(8,128)} %basis_hbm.1) | copy-start | bytes 3145732
  2.5 1.0 %copy-start.1 = (f32[1024,128]{1,0:T(8,128)S(1)}, f32[1024,128]{1,0:T(8,128)}, u32[]{:S(2)}) copy-start(f32[1024,128]{1,0:T(8,128)} %sketch_hbm.1) | copy-start | bytes 1572868
  3.6 0.9 %copy-start.2 = (f32[8,32,128]{2,1,0:T(8,128)S(1)}, f32[8,32,128]{2,1,0:T(8,128)}, u32[]{:S(2)}) copy-start(f32[8,32,128]{2,1,0:T(8,128)} %krylov_hbm.1) | copy-start | bytes 393220

commit v2 on v1

--- a/solution.py
+++ b/solution.py
@@ -69,13 +69,18 @@
 
     barrier = pltpu.get_barrier_semaphore()
 
-    def greet(i, carry):
-        pl.semaphore_signal(
-            barrier, inc=1, device_id=at(lax.rem(me + i, ndev)), device_id_type=MESH
-        )
-        return carry
-
-    lax.fori_loop(1, ndev, greet, 0)
+    def over(count, first, self_index, action):
+        def step(i, carry):
+            action(lax.rem(self_index + i, count))
+            return carry
+
+        lax.fori_loop(first, count, step, 0)
+
+    def greet(where):
+        pl.semaphore_signal(barrier, inc=1, device_id=where, device_id_type=MESH)
+
+    over(ng, 1, g, lambda p: greet((b, p)))
+    over(nb, 1, b, lambda p: greet((p, g)))
 
     for copy in copies[:3]:
         copy.wait()
@@ -86,35 +91,27 @@
     geo[...] = mine
     src_geo[g] = mine
     tgt_geo[b] = mine
-    copies[3].wait()
-    pl.semaphore_wait(barrier, ndev - 1)
-
-    def geo_copy(peer, slot):
-        return remote(geo, src_geo.at[slot], geo_send.at[peer], geo_recv.at[slot], (b, peer))
-
-    def tgt_copy(peer, slot):
-        return remote(geo, tgt_geo.at[slot], tgt_send.at[peer], tgt_recv.at[slot], (peer, g))
-
-    def w_copy(peer, slot):
-        return remote(
-            weights.at[g], weights.at[slot], w_send.at[peer], w_recv.at[slot], (b, peer)
-        )
-
-    def over(count, first, self_index, action):
-        def step(i, carry):
-            action(lax.rem(self_index + i, count))
-            return carry
-
-        lax.fori_loop(first, count, step, 0)
-
-    over(nb, 1, b, lambda p: tgt_copy(p, b).start())
-    over(ng, 1, g, lambda p: geo_copy(p, g).start())
-    over(ng, 1, g, lambda p: w_copy(p, g).start())
-
     copies[4].wait()
     high, low = split(sketch[...])
     sk_high[...] = high
     sk_low[...] = low
+    copies[3].wait()
+    pl.semaphore_wait(barrier, ng + nb - 2)
+
+    def geo_copy(peer, slot):
+        return remote(geo, src_geo.at[slot], geo_send.at[peer], geo_recv.at[slot], (b, peer))
+
+    def tgt_copy(peer, slot):
+        return remote(geo, tgt_geo.at[slot], tgt_send.at[peer], tgt_recv.at[slot], (peer, g))
+
+    def w_copy(peer, slot):
+        return remote(
+            weights.at[g], weights.at[slot], w_send.at[peer], w_recv.at[slot], (b, peer)
+        )
+
+    over(nb, 1, b, lambda p: tgt_copy(p, b).start())
+    over(ng, 1, g, lambda p: geo_copy(p, g).start())
+    over(ng, 1, g, lambda p: w_copy(p, g).start())
 
     over(nb, 1, b, lambda p: tgt_copy(p, p).wait_recv())
     for k in range(nb):
@@ -227,7 +224,23 @@
             sk_full.at[tile], sk_full.at[slot], ag_send.at[peer], ag_recv.at[slot], at(base + peer)
         )
 
-    over(ndev, 1, me, lambda p: rs_copy(p, me).start())
+    def far_first(count, width, index, action):
+        low = lax.rem(index, width) < width // 2
+
+        def step(i, carry):
+            along = i // (count // width)
+            other = lax.rem(i, count // width)
+            p = other * width + jnp.where(low, width - 1 - along, along)
+
+            @pl.when(p != index)
+            def _():
+                action(p)
+
+            return carry
+
+        lax.fori_loop(0, count, step, 0)
+
+    far_first(ndev, ng, me, lambda p: rs_copy(p, me).start())
     sk_in[me] = sk_part[tile]
     copies[5].wait()
     copies[6].wait()
@@ -245,7 +258,7 @@
     else:
         summed = lax.fori_loop(0, ndev // reach, add_tiles, jnp.zeros((8, 128), F32))
     sk_full[tile] = summed
-    over(tiles, 1, tile, lambda p: ag_copy(p, tile).start())
+    far_first(tiles, min(ng, tiles), tile, lambda p: ag_copy(p, tile).start())
     over(tiles, 1, tile, lambda p: ag_copy(p, p).wait_recv())
 
     lanes = lax.broadcasted_iota(jnp.int32, (8, 128), 1)
@@ -291,6 +304,27 @@
     over(tiles, 1, tile, lambda p: ag_copy(p, tile).wait_send())
 
 
+def place_kernel(count, *refs):
+    sems = refs[2 * count]
+    outward = [pltpu.make_async_copy(refs[k], refs[count + k], sems.at[k]) for k in range(count)]
+    for copy in outward:
+        copy.start()
+    for copy in outward:
+        copy.wait()
+
+
+def place(arrays):
+    count = len(arrays)
+    return pl.pallas_call(
+        functools.partial(place_kernel, count),
+        out_shape=tuple(jax.ShapeDtypeStruct(a.shape, a.dtype) for a in arrays),
+        in_specs=[pl.BlockSpec(memory_space=pltpu.VMEM)] * count,
+        out_specs=(pl.BlockSpec(memory_space=pltpu.HBM),) * count,
+        scratch_shapes=[pltpu.SemaphoreType.DMA((count,))],
+        compiler_params=pltpu.CompilerParams(vmem_limit_bytes=1024 * 1024),
+    )(*arrays)
+
+
 def shards(nb, ng, points, labels, shape_scale, krylov_basis, sketch, sketched_basis):
     own = points.shape[1]
     vectors, systems, _ = krylov_basis.shape
@@ -300,9 +334,16 @@
     assert ndev % tiles == 0
     vmem = pltpu.VMEM
     dma = pltpu.SemaphoreType.DMA
-    hbm = pl.BlockSpec(memory_space=pl.ANY)
+    hbm = pl.BlockSpec(memory_space=pltpu.HBM)
     out = pl.BlockSpec(memory_space=pltpu.VMEM)
-    next_vector, coefficients, sketch_next, norms = pl.pallas_call(
+    operands = [
+        pltpu.with_memory_space_constraint(operand, pltpu.HBM)
+        for operand in (
+            points, labels.reshape(1, own), shape_scale.reshape(1, own),
+            krylov_basis, sketch, sketched_basis,
+        )
+    ]
+    results = pl.pallas_call(
         functools.partial(step_kernel, nb, ng),
         out_shape=(
             jax.ShapeDtypeStruct((systems, own), F32),
@@ -331,10 +372,8 @@
         compiler_params=pltpu.CompilerParams(
             collective_id=0, has_side_effects=True, vmem_limit_bytes=48 * 1024 * 1024
         ),
-    )(
-        points, labels.reshape(1, own), shape_scale.reshape(1, own),
-        krylov_basis, sketch, sketched_basis,
-    )
+    )(*operands)
+    next_vector, coefficients, sketch_next, norms = place(results)
     return (next_vector, coefficients, sketch_next, norms.reshape(systems))
 
 

time: 37.1 us -> 29.5 us (0.80)
  local copies, waits for them, and re-layouts: 6.2 us -> 0 us
  Pallas kernels: 30 us -> 28.7 us
    unnamed x16 -> x0, local copies, waits for them, and re-layouts: 6.2 us -> none
    pallas_call x1, Pallas kernels: 30 us -> 28 us  [shards(): pl.pallas_call(functools.partial(step_kernel, nb, ng), out_shape=(jax.Sha...]
    pallas_call x0 -> x1, Pallas kernels: none -> 0.7 us  [place(): pl.pallas_call(functools.partial(place_kernel, count), out_shape=tuple((j...]
where the time goes in v2:
time: 29.5 us; the launch traced here: 29.3 us
  Pallas kernels  28.7 us (97%)
  between operations  0.64 us (2%)
    pallas_call x1, Pallas kernels, shards(): pl.pallas_call(functools.partial(step_kernel, nb, ng), out_shape=(jax.Sha...  28 us
    pallas_call x1, Pallas kernels, place(): pl.pallas_call(functools.partial(place_kernel, count), out_shape=tuple((j...  0.7 us

profile of v2, /device:TPU:0, one launch (start us, length us, event | category | flops | bytes accessed | tf_op | source)
XLA Modules:
  0.0 29.3 jit_solution(17476549592960089395)
XLA Ops:
  0.6 28.0 %shard_map.93 = (f32[32,128]{1,0:T(8,128)S(1)}, f32[8,32]{1,0:T(8,128)S(1)}, f32[32,1024]{1,0:T(8,128)S(1)}, f32[1,32]{1,0:T(1,128)S(1)}) custom-call(f32[3,128]{1,0:T(4,128)} %points_hbm.1, s32[1,128]{1,0:T(1,128)} %bitcast.3, f32[1,128]{1,0:T(1,128)} %bitcast.4, f32[8,32,128]{2,1,0:T(8,128)} %krylov_hbm.1, f32[1024,128]{1,0:T(8,128)} %sketch_hbm.1, ...), custom_call_target="tpu_custom_call" | custom-call | tf_op jit(solution)/shard_map/pallas_call | solution.py:346
  28.6 0.7 %shard_map.94 = (f32[32,128]{1,0:T(8,128)}, f32[8,32]{1,0:T(8,128)}, f32[32,1024]{1,0:T(8,128)}, f32[1,32]{1,0:T(1,128)}) custom-call(f32[32,128]{1,0:T(8,128)S(1)} %get-tuple-element.12.refs_0_, f32[8,32]{1,0:T(8,128)S(1)} %get-tuple-element.13.refs_1_, f32[32,1024]{1,0:T(8,128)S(1)} %get-tuple-element.14.refs_2_, f32[1,32]{1,0:T(1,128)S(1)} %get-tuple-element.15.refs_3_), custom_call_target="tpu_custom_call" | custom-call | tf_op jit(solution)/shard_map/pallas_call | solution.py:318

commit v3 on v2

--- a/solution.py
+++ b/solution.py
@@ -91,28 +91,44 @@
     geo[...] = mine
     src_geo[g] = mine
     tgt_geo[b] = mine
+    copies[3].wait()
+    pl.semaphore_wait(barrier, ng + nb - 2)
+
+    def geo_copy(peer, slot):
+        return remote(geo, src_geo.at[slot], geo_send.at[peer], geo_recv.at[slot], (b, peer))
+
+    def tgt_copy(peer, slot):
+        return remote(geo, tgt_geo.at[slot], tgt_send.at[peer], tgt_recv.at[slot], (peer, g))
+
+    def w_copy(peer, slot):
+        return remote(
+            weights.at[g], weights.at[slot], w_send.at[peer], w_recv.at[slot], (b, peer)
+        )
+
+    def far_first(count, width, index, action):
+        low = lax.rem(index, width) < width // 2
+
+        def step(i, carry):
+            along = i // (count // width)
+            other = lax.rem(i, count // width)
+            p = other * width + jnp.where(low, width - 1 - along, along)
+
+            @pl.when(p != index)
+            def _():
+                action(p)
+
+            return carry
+
+        lax.fori_loop(0, count, step, 0)
+
+    over(nb, 1, b, lambda p: tgt_copy(p, b).start())
+    far_first(ng, ng, g, lambda p: geo_copy(p, g).start())
+    far_first(ng, ng, g, lambda p: w_copy(p, g).start())
+
     copies[4].wait()
     high, low = split(sketch[...])
     sk_high[...] = high
     sk_low[...] = low
-    copies[3].wait()
-    pl.semaphore_wait(barrier, ng + nb - 2)
-
-    def geo_copy(peer, slot):
-        return remote(geo, src_geo.at[slot], geo_send.at[peer], geo_recv.at[slot], (b, peer))
-
-    def tgt_copy(peer, slot):
-        return remote(geo, tgt_geo.at[slot], tgt_send.at[peer], tgt_recv.at[slot], (peer, g))
-
-    def w_copy(peer, slot):
-        return remote(
-            weights.at[g], weights.at[slot], w_send.at[peer], w_recv.at[slot], (b, peer)
-        )
-
-    over(nb, 1, b, lambda p: tgt_copy(p, b).start())
-    over(ng, 1, g, lambda p: geo_copy(p, g).start())
-    over(ng, 1, g, lambda p: w_copy(p, g).start())
-
     over(nb, 1, b, lambda p: tgt_copy(p, p).wait_recv())
     for k in range(nb):
         turned = jnp.transpose(tgt_geo[k])
@@ -126,9 +142,9 @@
         return pl.ds(pl.multiple_of(p * own, own), own)
 
     def kernel_block(i, carry):
-        p = lax.rem(g + i, ng)
-
-        @pl.when(i > 0)
+        p = jnp.where(g < ng // 2, i, ng - 1 - i)
+
+        @pl.when(p != g)
         def _():
             geo_copy(p, p).wait_recv()
 
@@ -144,46 +160,43 @@
             interior = (q + q + ss) * (inverse * inverse)
             value = jnp.where(tgl[rows, :] > 0.5, interior, q) * inverse
             value_high, value_low = split(value)
-            k_high[rows, columns(p)] = value_high
-            k_low[rows, columns(p)] = value_low
+            k_high[rows, columns(i)] = value_high
+            k_low[rows, columns(i)] = value_low
         return carry
 
     lax.fori_loop(0, ng, kernel_block, 0)
 
     def weight_block(i, carry):
-        p = lax.rem(g + i, ng)
-
-        @pl.when(i > 0)
+        p = jnp.where(g < ng // 2, i, ng - 1 - i)
+
+        @pl.when(p != g)
         def _():
             w_copy(p, p).wait_recv()
 
         w_high, w_low = split(weights[p])
-        w_cat[0:systems, columns(p)] = w_high
-        w_cat[systems : 2 * systems, columns(p)] = w_low
+        w_cat[0:systems, columns(i)] = w_high
+        w_cat[systems : 2 * systems, columns(i)] = w_low
         return carry
 
-    lax.fori_loop(0, ng, weight_block, 0)
-
-    width = min(ng, 8) * own
-    chunks = (ng * own) // width
+    batch = min(ng // 2, 8)
+    width = batch * own
 
     def product(c):
+        lax.fori_loop(c * batch, (c + 1) * batch, weight_block, 0)
         cols = pl.ds(pl.multiple_of(c * width, width), width)
         both = nt_dot(w_cat[:, cols], k_high[:, cols])
         rest = nt_dot(w_cat[0:systems, cols], k_low[:, cols])
         return both[0:systems] + both[systems:] + rest
 
-    if chunks == 1:
-        total = product(0)
-    else:
-        acc[...] = jnp.zeros_like(acc)
+    acc[...] = product(0)
+    if ng // batch > 2:
 
         def add_chunk(c, carry):
             acc[...] += product(c)
             return carry
 
-        lax.fori_loop(0, chunks, add_chunk, 0)
-        total = acc[...]
+        lax.fori_loop(1, ng // batch - 1, add_chunk, 0)
+    total = acc[...] + product(ng // batch - 1)
     for k in range(nb):
         part[k] = total[:, k * own : (k + 1) * own]
 
@@ -223,22 +236,6 @@
         return remote(
             sk_full.at[tile], sk_full.at[slot], ag_send.at[peer], ag_recv.at[slot], at(base + peer)
         )
-
-    def far_first(count, width, index, action):
-        low = lax.rem(index, width) < width // 2
-
-        def step(i, carry):
-            along = i // (count // width)
-            other = lax.rem(i, count // width)
-            p = other * width + jnp.where(low, width - 1 - along, along)
-
-            @pl.when(p != index)
-            def _():
-                action(p)
-
-            return carry
-
-        lax.fori_loop(0, count, step, 0)
 
     far_first(ndev, ng, me, lambda p: rs_copy(p, me).start())
     sk_in[me] = sk_part[tile]

time: 29.5 us -> 28.7 us (0.973)
  Pallas kernels: 28.7 us -> 27.9 us
    pallas_call x1, Pallas kernels: 28 us -> 27.2 us  [shards(): pl.pallas_call(functools.partial(step_kernel, nb, ng), out_shape=(jax.Sha...]
where the time goes in v3:
time: 28.7 us; the launch traced here: 28.5 us
  Pallas kernels  27.9 us (97%)
  between operations  0.64 us (2%)
    pallas_call x1, Pallas kernels, shards(): pl.pallas_call(functools.partial(step_kernel, nb, ng), out_shape=(jax.Sha...  27.2 us
    pallas_call x1, Pallas kernels, place(): pl.pallas_call(functools.partial(place_kernel, count), out_shape=tuple((j...  0.7 us

profile of v3, /device:TPU:0, one launch (start us, length us, event | category | flops | bytes accessed | tf_op | source)
XLA Modules:
  0.0 28.5 jit_solution(3786624520684727493)
XLA Ops:
  0.6 27.2 %shard_map.93 = (f32[32,128]{1,0:T(8,128)S(1)}, f32[8,32]{1,0:T(8,128)S(1)}, f32[32,1024]{1,0:T(8,128)S(1)}, f32[1,32]{1,0:T(1,128)S(1)}) custom-call(f32[3,128]{1,0:T(4,128)} %points_hbm.1, s32[1,128]{1,0:T(1,128)} %bitcast.3, f32[1,128]{1,0:T(1,128)} %bitcast.4, f32[8,32,128]{2,1,0:T(8,128)} %krylov_hbm.1, f32[1024,128]{1,0:T(8,128)} %sketch_hbm.1, ...), custom_call_target="tpu_custom_call" | custom-call | tf_op jit(solution)/shard_map/pallas_call | solution.py:343
  27.8 0.7 %shard_map.94 = (f32[32,128]{1,0:T(8,128)}, f32[8,32]{1,0:T(8,128)}, f32[32,1024]{1,0:T(8,128)}, f32[1,32]{1,0:T(1,128)}) custom-call(f32[32,128]{1,0:T(8,128)S(1)} %get-tuple-element.12.refs_0_, f32[8,32]{1,0:T(8,128)S(1)} %get-tuple-element.13.refs_1_, f32[32,1024]{1,0:T(8,128)S(1)} %get-tuple-element.14.refs_2_, f32[1,32]{1,0:T(1,128)S(1)} %get-tuple-element.15.refs_3_), custom_call_target="tpu_custom_call" | custom-call | tf_op jit(solution)/shard_map/pallas_call | solution.py:315

commit v4 on v3

--- a/solution.py
+++ b/solution.py
@@ -64,9 +64,6 @@
         pltpu.make_async_copy(krylov_hbm, krylov, local_sem.at[5]),
         pltpu.make_async_copy(basis_hbm, basis, local_sem.at[6]),
     ]
-    for copy in copies:
-        copy.start()
-
     barrier = pltpu.get_barrier_semaphore()
 
     def over(count, first, self_index, action):
@@ -74,13 +71,15 @@
             action(lax.rem(self_index + i, count))
             return carry
 
-        lax.fori_loop(first, count, step, 0)
+        lax.fori_loop(first, count, step, 0, unroll=count <= 32)
 
     def greet(where):
         pl.semaphore_signal(barrier, inc=1, device_id=where, device_id_type=MESH)
 
     over(ng, 1, g, lambda p: greet((b, p)))
     over(nb, 1, b, lambda p: greet((p, g)))
+    for copy in copies:
+        copy.start()
 
     for copy in copies[:3]:
         copy.wait()
@@ -119,7 +118,7 @@
 
             return carry
 
-        lax.fori_loop(0, count, step, 0)
+        lax.fori_loop(0, count, step, 0, unroll=count <= 32)
 
     over(nb, 1, b, lambda p: tgt_copy(p, b).start())
     far_first(ng, ng, g, lambda p: geo_copy(p, g).start())

time: 28.7 us -> 28.3 us (0.986)
  Pallas kernels: 27.9 us -> 27.3 us
    pallas_call x1, Pallas kernels: 27.2 us -> 26.6 us  [shards(): pl.pallas_call(functools.partial(step_kernel, nb, ng), out_shape=(jax.Sha...]
where the time goes in v4:
time: 28.3 us; the launch traced here: 27.9 us
  Pallas kernels  27.3 us (96%)
  between operations  0.64 us (2%)
    pallas_call x1, Pallas kernels, shards(): pl.pallas_call(functools.partial(step_kernel, nb, ng), out_shape=(jax.Sha...  26.6 us
    pallas_call x1, Pallas kernels, place(): pl.pallas_call(functools.partial(place_kernel, count), out_shape=tuple((j...  0.7 us

profile of v4, /device:TPU:0, one launch (start us, length us, event | category | flops | bytes accessed | tf_op | source)
XLA Modules:
  0.0 27.9 jit_solution(9328777822660983356)
XLA Ops:
  0.6 26.6 %shard_map.93 = (f32[32,128]{1,0:T(8,128)S(1)}, f32[8,32]{1,0:T(8,128)S(1)}, f32[32,1024]{1,0:T(8,128)S(1)}, f32[1,32]{1,0:T(1,128)S(1)}) custom-call(f32[3,128]{1,0:T(4,128)} %points_hbm.1, s32[1,128]{1,0:T(1,128)} %bitcast.3, f32[1,128]{1,0:T(1,128)} %bitcast.4, f32[8,32,128]{2,1,0:T(8,128)} %krylov_hbm.1, f32[1024,128]{1,0:T(8,128)} %sketch_hbm.1, ...), custom_call_target="tpu_custom_call" | custom-call | tf_op jit(solution)/shard_map/pallas_call | solution.py:342
  27.2 0.7 %shard_map.94 = (f32[32,128]{1,0:T(8,128)}, f32[8,32]{1,0:T(8,128)}, f32[32,1024]{1,0:T(8,128)}, f32[1,32]{1,0:T(1,128)}) custom-call(f32[32,128]{1,0:T(8,128)S(1)} %get-tuple-element.12.refs_0_, f32[8,32]{1,0:T(8,128)S(1)} %get-tuple-element.13.refs_1_, f32[32,1024]{1,0:T(8,128)S(1)} %get-tuple-element.14.refs_2_, f32[1,32]{1,0:T(1,128)S(1)} %get-tuple-element.15.refs_3_), custom_call_target="tpu_custom_call" | custom-call | tf_op jit(solution)/shard_map/pallas_call | solution.py:314
